TPU v7x, 32 devices: a whole 2x2x4 slice. The times are simulated.
32 devices in a mesh: dp: 4 (over y, x), mp: 8 (over z, core).
Axes of the slice: x: 2, y: 2, z: 4, core: 2. Of those that a mesh axis runs over, the one named last changes fastest.
Arguments:
- data_rows: bfloat16 [16384, 2048], P(('dp', 'mp')), may hold values from -32 to 32
- centroids: bfloat16 [12288, 2048], P('mp'), may hold values from -0.75 to 0.75
- block_mask: int32 [8, 128], P(None, ('dp', 'mp')), may hold values from 0 to 1, as said below
- lower_bound: float32 [8, 16384], P(None, ('dp', 'mp')), may hold values from 0 to 4
Outputs:
- new_centroids: float32 [12288, 2048], P(('mp', 'dp'))
- centroid_shift: float32 [12288], P(('mp', 'dp'))
- log_norm: float32 [16384], P(('dp', 'mp'))
- new_lower: float32 [8, 16384], P(None, ('dp', 'mp'))
Inputs may be any that keep to these rules, and one draw needn't show every extreme that they name: `block_mask`: within the 4 blocks of one device (aligned runs along the last dimension), at most 1 are 1 for each shard; for some shard every device has exactly 1.
All inputs are finite; a program needn't handle non-finite values.
Results may differ from a plain program's by a relative error of at most 0.0011.
Values may be sent and summed in bfloat16 or wider, within the bound.
A program may use at most 128 MiB of HBM per device.

v0:
```python
import math

import jax
import jax.numpy as jnp
from jax import lax
from jax.sharding import PartitionSpec as P

BLOCK = 128
SLOTS = 1


def pack_codes(mask_dev, slot_total):
    block_count = mask_dev.shape[1]
    block_rank = jnp.cumsum(mask_dev, axis=1) - 1
    slot_ids = jnp.arange(slot_total, dtype=jnp.int32)
    chosen = (mask_dev[:, None, :] == 1) & (block_rank[:, None, :] == slot_ids[None, :, None])
    labels = jnp.arange(1, block_count + 1, dtype=jnp.int32)
    return jnp.sum(jnp.where(chosen, labels[None, None, :], 0), axis=2)


def slot_marks(slot_codes, block_count):
    labels = jnp.arange(1, block_count + 1, dtype=jnp.int32)
    return slot_codes[:, :, None] == labels[None, None, :]


def on_device(data_rows, centroids, block_mask, lower_bound):
    feat = data_rows.shape[1]
    block_count = data_rows.shape[0] // BLOCK
    shard_count = lax.axis_size("mp")
    sharpness = 4.0 / math.sqrt(feat)
    slot_codes = pack_codes(block_mask, SLOTS)
    row_blocks = data_rows.reshape(block_count, BLOCK, feat)
    outgoing = jnp.take(row_blocks, jnp.maximum(slot_codes - 1, 0), axis=0)
    outgoing = jnp.where((slot_codes > 0)[:, :, None, None], outgoing, jnp.zeros_like(outgoing))
    cent_norm = jnp.sum(jnp.square(centroids.astype(jnp.float32)), axis=1)
    piece_rows = lax.all_to_all(outgoing, "mp", split_axis=0, concat_axis=0, tiled=True)
    piece_codes = lax.all_to_all(
        slot_codes.astype(jnp.bfloat16), "mp", split_axis=0, concat_axis=0, tiled=True
    )
    products = jnp.einsum(
        "sbif,kf->sbik", piece_rows, centroids, preferred_element_type=jnp.float32
    )
    scores = sharpness * (2.0 * products - cent_norm)
    is_valid = (piece_codes > 0)[:, :, None]
    best = jnp.max(scores, axis=3)
    row_top = jnp.where(is_valid, best, -1e30)
    row_mass = jnp.where(is_valid, jnp.sum(jnp.exp(scores - best[..., None]), axis=3), 0.0)
    got_rows, got_codes, scores, row_top, row_mass = (
        piece_rows,
        piece_codes,
        scores,
        row_top,
        row_mass,
    )
    back_top, back_mass = (
        lax.all_to_all(row_top, "mp", split_axis=0, concat_axis=0, tiled=True),
        lax.all_to_all(row_mass, "mp", split_axis=0, concat_axis=0, tiled=True),
    )
    is_slot = slot_marks(slot_codes, block_count)
    block_top = jnp.max(jnp.where(is_slot[..., None], back_top[:, :, None, :], -1e30), axis=(0, 1))
    ceiling = jnp.maximum(block_top, 0.0)
    spread = back_mass[:, :, None, :] * jnp.exp(back_top[:, :, None, :] - ceiling[None, None])
    block_mass = jnp.sum(jnp.where(is_slot[..., None], spread, 0.0), axis=(0, 1))
    row_norm = ceiling + jnp.log(jnp.exp(-ceiling) + block_mass)
    log_norm = row_norm.reshape(-1)
    sent_norm = jnp.sum(jnp.where(is_slot[..., None], row_norm[None, None], 0.0), axis=2)
    slot_norm = lax.all_to_all(sent_norm, "mp", split_axis=0, concat_axis=0, tiled=True)
    is_valid = (got_codes > 0)[:, :, None, None]
    weight = jnp.where(is_valid, jnp.exp(scores - slot_norm[..., None]), 0.0)
    counts = jnp.sum(weight, axis=(0, 1, 2))
    weight_half = weight.astype(jnp.bfloat16)
    weighted = jnp.einsum(
        "sbik,sbif->kf", weight_half, got_rows, preferred_element_type=jnp.float32
    )
    part_sums, part_counts = (
        lax.psum_scatter(weighted, "dp", scatter_dimension=0, tiled=True),
        lax.psum_scatter(counts, "dp", scatter_dimension=0, tiled=True),
    )
    own_width = part_sums.shape[0]
    old_cents = lax.dynamic_slice_in_dim(
        centroids, lax.axis_index("dp") * own_width, own_width, 0
    ).astype(jnp.float32)
    updated = (part_sums + old_cents) / (part_counts[:, None] + 1.0)
    movement = jnp.sqrt(jnp.sum(jnp.square(updated - old_cents), axis=1) + 1.0)
    shard_peaks = lax.all_gather(jnp.max(movement)[None], ("dp", "mp"), axis=0, tiled=True)
    shard_peak = jnp.max(shard_peaks.reshape(-1, shard_count), axis=0)
    new_lower = lower_bound - shard_peak[:, None]
    return (updated, movement, log_norm, new_lower)


def solution(mesh):
    placed = (P(("dp", "mp"), None), P("mp", None), P(None, ("dp", "mp")), P(None, ("dp", "mp")))
    return jax.shard_map(
        on_device,
        mesh=mesh,
        in_specs=placed,
        out_specs=(P(("mp", "dp"), None), P(("mp", "dp")), P(("dp", "mp")), P(None, ("dp", "mp"))),
        check_vma=False,
    )
```

profile of v0, /device:TPU:0, one launch (start us, length us, event | category | flops | bytes accessed | tf_op | source)
XLA Modules:
  0.0 350.0 jit_solution(6557733593494368783)
XLA Ops:
  7.2 0.9 reduce_window_sum.11
  8.0 0.8 select_reduce_fusion.3
  9.5 6.4 %all-to-all-start = ((bf16[8,1,1]{2,1,0:T(2,128)(2,1)}), bf16[8,1,1]{2,1,0:T(2,128)(2,1)S(1)}, u32[]{:S(2)}, u32[]{:S(2)}) async-start(bf16[8,1,1]{2,1,0:T(2,128)(2,1)} %copy.16), calls=%async_computation | async-start | bytes 8192 | tf_op jit(solution)/shard_map/all_to_all | solution.py:37
  15.9 2.7 gather_fusion
  18.6 4.6 %fusion.8 = bf16[8,1,128,2048]{3,2,1,0:T(8,128)(2,1)} fusion(bf16[8,128,2048]{2,1,0:T(8,128)(2,1)} %gather_fusion, pred[8]{0:T(512)(128)(4,1)S(1)} %get-tuple-element.13, pred[8]{0:T(512)(128)(4,1)S(1)} %get-tuple-element.12), kind=kLoop, calls=%fused_computation.13 | loop fusion | flops 4194304 | bytes 8388624 | tf_op jit(solution)/shard_map/jit(_where)/select_n | solution.py:34
  23.3 5.1 %all-to-all-start.1 = ((bf16[8,1,128,2048]{3,2,1,0:T(8,128)(2,1)}), bf16[8,1,128,2048]{3,2,1,0:T(8,128)(2,1)}, u32[]{:S(2)}, u32[]{:S(2)}) async-start(bf16[8,1,128,2048]{3,2,1,0:T(8,128)(2,1)} %fusion.8), calls=%async_computation.1 | async-start | bytes 8388608 | tf_op jit(solution)/shard_map/all_to_all | solution.py:36
  28.4 4.1 %multiply_reduce_fusion = f32[1536]{0:T(1024)S(1)} fusion(bf16[1536,2048]{1,0:T(8,128)(2,1)} %param.5), kind=kLoop, calls=%fused_computation.1 | loop fusion | flops 9435648 | bytes 6297600 | tf_op jit(solution)/shard_map/reduce_sum | solution.py:35
  32.7 89.8 %all-to-all-done.1 = bf16[8,1,128,2048]{3,2,1,0:T(8,128)(2,1)} async-done(((bf16[8,1,128,2048]{3,2,1,0:T(8,128)(2,1)}), bf16[8,1,128,2048]{3,2,1,0:T(8,128)(2,1)}, u32[]{:S(2)}, u32[]{:S(2)}) %all-to-all-start.1) | async-done | bytes 4194336 | tf_op jit(solution)/shard_map/all_to_all | solution.py:36
  122.5 10.6 %fusion.23 = (f32[8,128]{1,0:T(8,128)S(1)}, f32[8,128,1536]{2,1,0:T(8,128)S(1)}) fusion(f32[1536]{0:T(1024)S(1)} %multiply_reduce_fusion, bf16[1536,2048]{1,0:T(8,128)(2,1)} %param.5, bf16[8,1,128,2048]{3,2,1,0:T(8,128)(2,1)} %all-to-all-done.1), kind=kOutput, calls=%fused_computation.50 | convolution fusion | flops 6448741376 | bytes 16787456 | tf_op jit(solution)/shard_map/sbif,kf->sbik/dot_general | solution.py:40
  133.0 2.6 copy-done.1
  135.6 1.0 exponential_reduce_fusion
  137.4 3.3 all-to-all-start.2
  140.8 5.4 %all-to-all-done.2 = f32[8,1,128]{2,1,0:T(1,128)S(1)} async-done(((f32[8,1,128]{2,1,0:T(1,128)}), f32[8,1,128]{2,1,0:T(1,128)S(1)}, u32[]{:S(2)}, u32[]{:S(2)}) %all-to-all-start.2) | async-done | bytes 4128 | tf_op jit(solution)/shard_map/all_to_all | solution.py:56
  146.1 3.3 all-to-all-start.3
  149.6 5.3 %all-to-all-done.3 = f32[8,1,128]{2,1,0:T(1,128)S(1)} async-done(((f32[8,1,128]{2,1,0:T(1,128)}), f32[8,1,128]{2,1,0:T(1,128)S(1)}, u32[]{:S(2)}, u32[]{:S(2)}) %all-to-all-start.3) | async-done | bytes 4128 | tf_op jit(solution)/shard_map/all_to_all | solution.py:57
  155.1 8.0 %all_to_all.26 = f32[8,1,128]{2,1,0:T(1,128)S(1)} all-to-all(f32[8,1,128]{2,1,0:T(1,128)S(1)} %bitcast.52), channel_id=1, replica_groups=mesh['dp'=4,'mp'=8] {'mp'}, dimensions={0} | all-to-all | bytes 8192 | tf_op jit(solution)/shard_map/all_to_all | solution.py:67
  163.0 13.2 %convolution_bitcast_fusion = f32[1536,2048]{1,0:T(8,128)} fusion(bf16[8,1,128,2048]{3,2,1,0:T(8,128)(2,1)} %all-to-all-done.1, f32[8,128,1536]{2,1,0:T(8,128)} %copy-done.1, f32[8,128]{1,0:T(8,128)S(1)} %bitcast.53, pred[8]{0:T(512)(128)(4,1)S(1)} %compare_reduce_fusion), kind=kOutput, calls=%fused_computation.2 | convolution fusion | flops 6447169536 | bytes 23072776 | tf_op jit(solution)/shard_map/sbik,sbif->kf/dot_general | solution.py:72
  178.1 3.9 %fusion.2 = f32[1536]{0:T(1024)S(1)} fusion(f32[8,128,1536]{2,1,0:T(8,128)} %copy-done.1, f32[8,128]{1,0:T(8,128)S(1)} %bitcast.54, pred[8]{0:T(512)(128)(4,1)S(1)} %compare_reduce_fusion), kind=kLoop, calls=%fused_computation.8 | loop fusion | flops 4717056 | bytes 6301704 | tf_op jit(solution)/shard_map/reduce_sum | solution.py:70
  182.0 10.8 %all-reduce.1 = f32[1536]{0:T(1024)S(1)} all-reduce(f32[1536]{0:T(1024)S(1)} %fusion.2), channel_id=3, replica_groups=mesh['dp'=4,'mp'=8] {'dp'}, use_global_device_ids=true, to_apply=%region_10.11.clone | all-reduce | flops 1536 | bytes 12288
  193.0 102.8 %reduce-scatter.2.cloned.1.call-done = f32[384,2048]{1,0:T(8,128)} async-done(((f32[1536,2048]{1,0:T(8,128)}), f32[384,2048]{1,0:T(8,128)}) %reduce-scatter.2.cloned.1.call-update) | async-done | bytes 3145744 | tf_op jit(solution)/shard_map/reduce_scatter | solution.py:76
  295.8 4.8 %fusion.11 = (f32[384]{0:T(512)S(1)}, f32[384,2048]{1,0:T(8,128)}) fusion(bf16[1536,2048]{1,0:T(8,128)(2,1)} %param.5, s32[]{:T(128)S(6)} %select_n.108, f32[384]{0:T(512)S(1)} %dynamic-slice_add_fusion, f32[384,2048]{1,0:T(8,128)} %reduce-scatter.2.cloned.1.call-done), kind=kLoop, calls=%fused_computation.18 | loop fusion | flops 4718208 | bytes 7867396 | tf_op jit(solution)/shard_map/reduce_sum | solution.py:84
  300.6 1.2 fusion.21
  301.7 0.8 dynamic-update-slice
  303.1 39.2 %all-reduce = f32[32]{0:T(128)S(1)} all-reduce(f32[32]{0:T(128)S(1)} %dynamic-update-slice), channel_id=1, replica_groups=mesh['dp'=4,'mp'=8] {'dp','mp'}, use_global_device_ids=true, to_apply=%add | all-reduce | flops 32 | bytes 256
  (30 shorter events, 4.7 us)
Async XLA Ops:
  7.2 8.7 %copy-start = (bf16[512,2048]{1,0:T(8,128)(2,1)S(1)}, bf16[512,2048]{1,0:T(8,128)(2,1)}, u32[]{:S(2)}) copy-start(bf16[512,2048]{1,0:T(8,128)(2,1)} %param.4) | copy-start | bytes 6291460
  9.5 13.8 %all-to-all-start = ((bf16[8,1,1]{2,1,0:T(2,128)(2,1)}), bf16[8,1,1]{2,1,0:T(2,128)(2,1)S(1)}, u32[]{:S(2)}, u32[]{:S(2)}) async-start(bf16[8,1,1]{2,1,0:T(2,128)(2,1)} %copy.16), calls=%async_computation | async-start | bytes 8192 | tf_op jit(solution)/shard_map/all_to_all | solution.py:37
  23.3 99.2 %all-to-all-start.1 = ((bf16[8,1,128,2048]{3,2,1,0:T(8,128)(2,1)}), bf16[8,1,128,2048]{3,2,1,0:T(8,128)(2,1)}, u32[]{:S(2)}, u32[]{:S(2)}) async-start(bf16[8,1,128,2048]{3,2,1,0:T(8,128)(2,1)} %fusion.8), calls=%async_computation.1 | async-start | bytes 8388608 | tf_op jit(solution)/shard_map/all_to_all | solution.py:36
  133.0 2.6 copy-start.1
  137.4 8.8 %all-to-all-start.2 = ((f32[8,1,128]{2,1,0:T(1,128)}), f32[8,1,128]{2,1,0:T(1,128)S(1)}, u32[]{:S(2)}, u32[]{:S(2)}) async-start(f32[8,1,128]{2,1,0:T(1,128)} %get-tuple-element.9), calls=%async_computation.2 | async-start | bytes 8192 | tf_op jit(solution)/shard_map/all_to_all | solution.py:56
  146.1 8.8 %all-to-all-start.3 = ((f32[8,1,128]{2,1,0:T(1,128)}), f32[8,1,128]{2,1,0:T(1,128)S(1)}, u32[]{:S(2)}, u32[]{:S(2)}) async-start(f32[8,1,128]{2,1,0:T(1,128)} %get-tuple-element.8), calls=%async_computation.3 | async-start | bytes 8192 | tf_op jit(solution)/shard_map/all_to_all | solution.py:57
  149.4 146.3 %reduce-scatter.2.cloned.1.call-start = ((), (), s32[]{:S(2)}) async-start(), calls=%async_computation.6 | async-start | bytes 15728640 | tf_op jit(solution)/shard_map/reduce_scatter | solution.py:76
  176.2 0.7 copy-start.3
  178.1 164.3 %copy-start.2 = (f32[8,512]{1,0:T(8,128)S(1)}, f32[8,512]{1,0:T(8,128)}, u32[]{:S(2)}) copy-start(f32[8,512]{1,0:T(8,128)} %param.7) | copy-start | bytes 49156
Sparse Core Ops, SparseCore 0:
  176.4 119.3 reduce-scatter.1
where the time goes:
time: 351 us; the launch traced here: 350 us
  waiting for transfers between devices  203 us (58%)
  blocking collectives  58 us (17%)
  other arithmetic  23.9 us (7%)
  matrix products  23.8 us (7%)
  starting transfers between devices  18.1 us (5%)
  between operations  14.8 us (4%)
  local copies, waits for them, and re-layouts  8.09 us (2%)
    reduce_scatter x1, waiting for transfers between devices, on_device(): lax.psum_scatter(weighted, 'dp', scatter_dimension=0, tiled=True)  103 us
    all_to_all x1, waiting for transfers between devices, on_device(): lax.all_to_all(outgoing, 'mp', split_axis=0, concat_axis=0, tiled=True)  89.8 us
    unnamed x2, blocking collectives  50.1 us
    dot_general x1, matrix products, on_device(): jnp.einsum('sbik,sbif->kf', weight_half, got_rows, preferred_element_type...  13.2 us
    dot_general x1, matrix products, on_device(): jnp.einsum('sbif,kf->sbik', piece_rows, centroids, preferred_element_type...  10.6 us
    all_to_all x1, blocking collectives, on_device(): lax.all_to_all(sent_norm, 'mp', split_axis=0, concat_axis=0, tiled=True)  7.95 us
  transfers between devices with their start and end apart: 5, of which 4 were waited for; matrix products, arithmetic and copies ran while one was open for 5% of the time, Pallas kernels for 0%

commit v1 on v0

v1 whole, which is shorter than its diff:
```python
import functools
import math

import jax
import jax.numpy as jnp
from jax import lax
from jax.experimental import pallas as pl
from jax.experimental.pallas import tpu as pltpu
from jax.sharding import PartitionSpec as P

BLOCK = 128
SLOTS = 1
LOW = -1e30
MESH = pl.DeviceIdType.MESH
NT = (((1,), (1,)), ((), ()))


def xor(a, b, limit):
    out, bit = 0, 1
    while bit < limit:
        out = out + (((a // bit) % 2) + ((b // bit) % 2)) % 2 * bit
        bit *= 2
    return out


def skip_bit(j, stride):
    return j % stride + (j // stride) * 2 * stride


def kernel(dims, out_rows, codes, cents, upd, mv2, lognorm,
           x, cl, cn, s, w, st, gst, nm, norm, ct, cr, sb, rb,
           bar_l, sem_bs, sem_br, sem_fs, sem_fr, sem_ss, sem_sr,
           sem_ms, sem_mr, sem_rs, sem_rr, sem_ns, sem_nr):
    n_dp, n_mp, feat, ks, sharp, nblk, stride, cols = dims
    group = n_dp // 2
    np_ = 2 * n_mp
    nc = feat // cols
    d, m = lax.axis_index("dp"), lax.axis_index("mp")
    core = m % 2

    def pick(a, b, which):
        return a * (1 - which) + b * which

    def mate_of(which):
        return pick(xor(d, 1, n_dp), xor(d, stride, n_dp), which)

    mate = mate_of(core)

    def red(j):
        return pick(xor(d, skip_bit(j, 1), n_dp), xor(d, skip_bit(j, stride), n_dp), core)

    def owner(p):
        g, t = p % 2, p // 2
        return {"dp": pick(d, mate, g), "mp": xor(m, t, n_mp)}

    def scorer(p):
        g, t = p % 2, p // 2
        return {"dp": pick(d, mate_of((core + t) % 2), g), "mp": xor(m, t, n_mp)}

    barrier = pltpu.get_barrier_semaphore()
    partners = [owner(p) for p in range(1, np_)]
    partners += [scorer(p) for p in range(1, np_) if p % 2 and (p // 2) % 2]
    partners += [{"dp": red(j), "mp": m} for j in range(1, group)]
    for device in partners:
        pl.semaphore_signal(barrier, inc=1, device_id=device, device_id_type=MESH)

    own = pltpu.make_async_copy(out_rows.at[0], x.at[0], bar_l.at[0])
    own.start()
    loads = []
    for j in range(group):
        c = pltpu.make_async_copy(cents.at[red(j)], cl.at[pl.ds(j * ks, ks)], bar_l.at[1 + j])
        c.start()
        loads.append(c)
    pl.semaphore_wait(barrier, len(partners))

    def block_copy(t):
        return pltpu.make_async_remote_copy(
            src_ref=out_rows.at[t], dst_ref=x.at[2 * t], send_sem=sem_bs.at[t],
            recv_sem=sem_br.at[t], device_id={"dp": d, "mp": xor(m, t, n_mp)}, device_id_type=MESH)

    def forward(t):
        return pltpu.make_async_remote_copy(
            src_ref=x.at[2 * t], dst_ref=x.at[2 * t + 1], send_sem=sem_fs.at[t],
            recv_sem=sem_fr.at[t], device_id={"dp": mate, "mp": m}, device_id_type=MESH)

    def stat_copy(p):
        return pltpu.make_async_remote_copy(
            src_ref=st.at[p], dst_ref=gst.at[p], send_sem=sem_ss.at[p],
            recv_sem=sem_sr.at[p], device_id=owner(p), device_id_type=MESH)

    def norm_copy(p):
        return pltpu.make_async_remote_copy(
            src_ref=nm.at[p // 2], dst_ref=norm.at[p], send_sem=sem_ms.at[p],
            recv_sem=sem_mr.at[p], device_id=scorer(p), device_id_type=MESH)

    def sum_copy(j, c):
        return pltpu.make_async_remote_copy(
            src_ref=sb.at[j - 1, c], dst_ref=rb.at[j - 1, c], send_sem=sem_rs.at[j - 1, c],
            recv_sem=sem_rr.at[j - 1, c], device_id={"dp": red(j), "mp": m}, device_id_type=MESH)

    def count_copy(j):
        return pltpu.make_async_remote_copy(
            src_ref=ct.at[pl.ds(j * ks, ks)], dst_ref=cr.at[j - 1], send_sem=sem_ns.at[j - 1],
            recv_sem=sem_nr.at[j - 1], device_id={"dp": red(j), "mp": m}, device_id_type=MESH)

    for t in range(1, n_mp):
        block_copy(t).start()

    for c in loads:
        c.wait()
    own.wait()

    step = 16

    def norm_rows(i, _):
        r = pl.ds(pl.multiple_of(i * step, step), step)
        v = cl[r, :].astype(jnp.float32)
        cn[r, :] = jnp.broadcast_to(jnp.sum(v * v, axis=1, keepdims=True), (step, BLOCK))
        return 0

    forward(0).start()
    lax.fori_loop(0, cl.shape[0] // step, norm_rows, 0)

    def score(p):
        prod = lax.dot_general(cl[...], x[p], NT, preferred_element_type=jnp.float32)
        sc = sharp * (2.0 * prod - cn[...])
        s[p] = sc
        top = jnp.max(sc, axis=0, keepdims=True)
        st[p, 0:1, :] = top
        st[p, 1:2, :] = jnp.sum(jnp.exp(sc - top), axis=0, keepdims=True)

    score(0)

    def body(i, _):
        @pl.when(i < n_mp)
        def _():
            block_copy(i).wait_recv()
            forward(i).start()
            score(2 * i)
            stat_copy(2 * i).start()

        forward(i - 1).wait_recv()
        score(2 * i - 1)
        stat_copy(2 * i - 1).start()
        return 0

    lax.fori_loop(1, n_mp + 1, body, 0)
    gst[0] = st[0]
    for p in range(1, np_):
        stat_copy(p).wait_recv()

    mine = [codes[t:t + 1, :] for t in range(n_mp)]
    slot = [jnp.full((1, BLOCK), -LOW, jnp.float32) for _ in range(n_mp)]
    for b in range(nblk):
        top = jnp.zeros((1, BLOCK), jnp.float32)
        for p in range(np_):
            top = jnp.maximum(top, jnp.where(mine[p // 2] == b + 1, gst[p, 0:1, :], LOW))
        total = jnp.exp(-top)
        for p in range(np_):
            part = gst[p, 1:2, :] * jnp.exp(jnp.minimum(gst[p, 0:1, :] - top, 0.0))
            total = total + jnp.where(mine[p // 2] == b + 1, part, 0.0)
        val = top + jnp.log(total)
        lognorm[b:b + 1, :] = val
        slot = [jnp.where(mine[t] == b + 1, val, slot[t]) for t in range(n_mp)]
    for t in range(n_mp):
        nm[t] = slot[t]
    for p in range(1, np_):
        norm_copy(p).start()
    norm[0] = slot[0]
    for p in range(1, np_):
        norm_copy(p).wait_recv()

    ct[...] = jnp.zeros_like(ct)

    def weigh(p, _):
        wt = jnp.exp(s[p] - norm[p])
        ct[...] += wt
        w[:, pl.ds(pl.multiple_of(p * BLOCK, BLOCK), BLOCK)] = wt.astype(jnp.bfloat16)
        return 0

    lax.fori_loop(0, np_, weigh, 0)

    def partial(j, c):
        at = pl.ds(pl.multiple_of(c * cols, cols), cols)
        return jnp.dot(w[j * ks:(j + 1) * ks, :], x[:, :, at].reshape(np_ * BLOCK, cols),
                       preferred_element_type=jnp.float32)

    for j in range(1, group):
        count_copy(j).start()

        def send(c, _):
            sb[j - 1, c] = partial(j, c)
            sum_copy(j, c).start()
            return 0

        lax.fori_loop(0, nc, send, 0)
    cnt = ct[:ks]
    for j in range(1, group):
        count_copy(j).wait_recv()
        cnt = cnt + cr[j - 1]
    ct[:ks] = jnp.broadcast_to(jnp.sum(cnt, axis=1, keepdims=True) + 1.0, (ks, BLOCK))
    mv2[...] = jnp.zeros_like(mv2)

    def finish(c, _):
        at = pl.ds(pl.multiple_of(c * cols, cols), cols)
        total = partial(0, c)
        for j in range(1, group):
            sum_copy(j, c).wait_recv()
            total = total + rb[j - 1, c]
        old = cl[:ks, at].astype(jnp.float32)
        new = (total + old) / ct[:ks, :1]
        upd[:, at] = new
        mv2[...] += jnp.broadcast_to(
            jnp.sum(jnp.square(new - old), axis=1, keepdims=True), (ks, BLOCK))
        return 0

    lax.fori_loop(0, nc, finish, 0)

    for p in range(1, np_):
        stat_copy(p).wait_send()
        norm_copy(p).wait_send()
    for t in range(n_mp):
        if t:
            block_copy(t).wait_send()
        forward(t).wait_send()
    for j in range(1, group):
        count_copy(j).wait_send()
        for c in range(nc):
            sum_copy(j, c).wait_send()


def on_device(data_rows, centroids, block_mask, lower_bound):
    n_rows, feat = data_rows.shape
    nblk = n_rows // BLOCK
    n_dp, n_mp = lax.axis_size("dp"), lax.axis_size("mp")
    m = lax.axis_index("mp")
    ks = centroids.shape[0] // n_dp
    group, np_ = n_dp // 2, 2 * n_mp
    kc = group * ks
    stride = math.isqrt(n_dp)
    cols = 512
    nc = feat // cols
    labels = jnp.arange(1, nblk + 1, dtype=jnp.int32)
    order = jnp.bitwise_xor(jnp.arange(n_mp, dtype=jnp.int32), m)
    slot_codes = jnp.sum(jnp.take(block_mask, order, axis=0) * labels[None], axis=1)
    outgoing = jnp.take(data_rows.reshape(nblk, BLOCK, feat), jnp.maximum(slot_codes - 1, 0), axis=0)
    codes = jnp.broadcast_to(slot_codes[:, None], (n_mp, BLOCK))
    dims = (n_dp, n_mp, feat, ks, 4.0 / math.sqrt(feat), nblk, stride, cols)
    f32, bf16 = jnp.float32, jnp.bfloat16
    dma = pltpu.SemaphoreType.DMA
    vm = pl.BlockSpec(memory_space=pltpu.VMEM)
    hbm = pl.BlockSpec(memory_space=pl.ANY)
    upd, mv2, lognorm = pl.pallas_call(
        functools.partial(kernel, dims),
        out_shape=(
            jax.ShapeDtypeStruct((ks, feat), f32),
            jax.ShapeDtypeStruct((ks, BLOCK), f32),
            jax.ShapeDtypeStruct((nblk, BLOCK), f32),
        ),
        in_specs=[hbm, vm, hbm],
        out_specs=(vm, vm, vm),
        scratch_shapes=[
            pltpu.VMEM((np_, BLOCK, feat), bf16),
            pltpu.VMEM((kc, feat), bf16),
            pltpu.VMEM((kc, BLOCK), f32),
            pltpu.VMEM((np_, kc, BLOCK), f32),
            pltpu.VMEM((kc, np_ * BLOCK), bf16),
            pltpu.VMEM((np_, 2, BLOCK), f32),
            pltpu.VMEM((np_, 2, BLOCK), f32),
            pltpu.VMEM((n_mp, 1, BLOCK), f32),
            pltpu.VMEM((np_, 1, BLOCK), f32),
            pltpu.VMEM((kc, BLOCK), f32),
            pltpu.VMEM((group - 1, ks, BLOCK), f32),
            pltpu.VMEM((group - 1, nc, ks, cols), f32),
            pltpu.VMEM((group - 1, nc, ks, cols), f32),
            dma((1 + group,)),
            dma((n_mp,)), dma((n_mp,)),
            dma((n_mp,)), dma((n_mp,)),
            dma((np_,)), dma((np_,)),
            dma((np_,)), dma((np_,)),
            dma((group - 1, nc)), dma((group - 1, nc)),
            dma((group - 1,)), dma((group - 1,)),
        ],
        compiler_params=pltpu.CompilerParams(
            collective_id=0, has_side_effects=True, vmem_limit_bytes=60 * 1024 * 1024),
    )(outgoing, codes, centroids.reshape(n_dp, ks, feat))
    movement = jnp.sqrt(mv2[:, 0] + 1.0)
    shard_peaks = lax.all_gather(jnp.max(movement)[None], ("dp", "mp"), axis=0, tiled=True)
    shard_peak = jnp.max(shard_peaks.reshape(-1, n_mp), axis=0)
    return upd, movement, lognorm.reshape(-1), lower_bound - shard_peak[:, None]


def solution(mesh):
    placed = (P(("dp", "mp"), None), P("mp", None), P(None, ("dp", "mp")), P(None, ("dp", "mp")))
    return jax.shard_map(
        on_device,
        mesh=mesh,
        in_specs=placed,
        out_specs=(P(("mp", "dp"), None), P(("mp", "dp")), P(("dp", "mp")), P(None, ("dp", "mp"))),
        check_vma=False,
    )
```

time: 351 us -> 214 us (0.61)
  waiting for transfers between devices: 203 us -> 0 us
  Pallas kernels: 0 us -> 157 us
  matrix products: 23.8 us -> 0 us
  blocking collectives: 58 us -> 38.8 us
  starting transfers between devices: 18.1 us -> 0 us
  other arithmetic: 23.9 us -> 7.27 us
  between operations: 14.8 us -> 0.71 us
    pallas_call x0 -> x1, Pallas kernels: none -> 157 us  [on_device(): pl.pallas_call(functools.partial(kernel, dims), out_shape=(jax.ShapeDtype...]
    reduce_scatter x1 -> x0, waiting for transfers between devices: 103 us -> none  [on_device(): lax.psum_scatter(weighted, 'dp', scatter_dimension=0, tiled=True)]
    all_to_all x4 -> x0, waiting for transfers between devices: 100 us -> none  [the longest x1 89.8 us: on_device(): lax.all_to_all(outgoing, 'mp', split_axis=0, concat_axis=0, tiled=True)]
    dot_general x2 -> x0, matrix products: 23.8 us -> none  [the longest x1 13.2 us: on_device(): jnp.einsum('sbik,sbif->kf', weight_half, got_rows, preferred_element_type...]
    all_to_all x4 -> x0, starting transfers between devices: 18.1 us -> none  [the longest x1 6.35 us: on_device(): lax.all_to_all(slot_codes.astype(jnp.bfloat16), 'mp', split_axis=0, conca...]
    reduce_sum x7 -> x1, other arithmetic: 14.7 us -> 0.18 us  [on_device(): jnp.sum(jnp.take(block_mask, order, axis=0) * labels[None], axis=1)]
    unnamed x2 -> x1, blocking collectives: 50.1 us -> 38.8 us
    all_to_all x1 -> x0, blocking collectives: 7.95 us -> none  [on_device(): lax.all_to_all(sent_norm, 'mp', split_axis=0, concat_axis=0, tiled=True)]
  transfers between devices with their start and end apart: 5 -> 0, of which waited for: 4 -> 0; matrix products, arithmetic and copies ran while one was open for 5% -> 0% of each run, Pallas kernels for 0% -> 0%
where the time goes in v1:
time: 214 us
  Pallas kernels  157 us (73%)
  blocking collectives  38.8 us (18%)
  local copies, waits for them, and re-layouts  10.2 us (5%)
  other arithmetic  7.27 us (3%)
    pallas_call x1, Pallas kernels, on_device(): pl.pallas_call(functools.partial(kernel, dims), out_shape=(jax.ShapeDtype...  157 us
    unnamed x1, blocking collectives  38.8 us
    unnamed x11, local copies, waits for them, and re-layouts  6.16 us
    select_n x1, other arithmetic, on_device(): jnp.take(data_rows.reshape(nblk, BLOCK, feat), jnp.maximum(slot_codes - 1...  4.57 us

profile of v1, /device:TPU:0, one launch (start us, length us, event | category | flops | bytes accessed | tf_op | source)
XLA Modules:
  0.0 213.7 jit_solution(17018995351290003033)
XLA Ops:
  0.6 0.0 copy-start
  0.7 0.9 copy.9
  1.6 0.6 gather_fusion
  2.2 0.2 multiply_reduce_fusion
  2.4 0.0 copy-done
  2.4 2.7 %gather_fusion.1 = bf16[8,128,2048]{2,1,0:T(8,128)(2,1)} fusion(bf16[4,128,2048]{2,1,0:T(8,128)(2,1)S(1)} %bitcast.6, s32[1024]{0:T(1024)S(1)} %pad_clamp_fusion), kind=kCustom, calls=%fused_computation.1 | custom fusion | bytes 8388640 | tf_op jit(solution)/shard_map/jit(_take)/gather | solution.py:246
  5.1 4.6 %broadcast_select_fusion.out_rows = bf16[8,128,2048]{2,1,0:T(8,128)(2,1)} fusion(bf16[8,128,2048]{2,1,0:T(8,128)(2,1)} %gather_fusion.1, pred[8]{0:T(512)(128)(4,1)S(1)} %broadcast_compare_fusion), kind=kLoop, calls=%fused_computation.2 | loop fusion | flops 2097152 | bytes 8388616 | tf_op jit(solution)/shard_map/jit(_take)/select_n | solution.py:246
  9.7 0.7 broadcast_in_dim.35.codes
  10.4 0.0 copy-start.1
  10.4 156.8 %shard_map.75 = (f32[384,2048]{1,0:T(8,128)}, f32[384,128]{1,0:T(8,128)}, f32[4,128]{1,0:T(4,128)}) custom-call(bf16[8,128,2048]{2,1,0:T(8,128)(2,1)} %broadcast_select_fusion.out_rows, s32[8,128]{1,0:T(8,128)} %broadcast_in_dim.35.codes, bf16[4,384,2048]{2,1,0:T(8,128)(2,1)} %bitcast.7), custom_call_target="tpu_custom_call" | custom-call | tf_op jit(solution)/shard_map/pallas_call | solution.py:253
  167.1 0.0 copy-start.2
  167.1 1.8 fusion
  168.9 0.8 dynamic-update-slice
  169.6 38.8 %all-reduce = f32[32]{0:T(128)S(1)} all-reduce(f32[32]{0:T(128)S(1)} %dynamic-update-slice), channel_id=1, replica_groups=mesh['dp'=4,'mp'=8] {'dp','mp'}, use_global_device_ids=true, to_apply=%add | all-reduce | flops 32 | bytes 256
  208.4 0.1 reshape.72
  208.6 0.0 copy-done.1
  208.6 0.7 broadcast_subtract_fusion
  209.2 3.9 %copy.13 = f32[384,2048]{1,0:T(8,128)} copy(f32[384,2048]{1,0:T(8,128)} %get-tuple-element.16) | data formatting | bytes 6291456
  213.1 0.0 copy-done.2
  213.1 0.6 copy.14
  (9 shorter events, 0.1 us)
Async XLA Ops:
  0.6 1.7 copy-start
  10.4 198.2 %copy-start.1 = (f32[8,512]{1,0:T(8,128)S(1)}, f32[8,512]{1,0:T(8,128)}, u32[]{:S(2)}) copy-start(f32[8,512]{1,0:T(8,128)} %param.7) | copy-start | bytes 49156
  167.1 46.0 %copy-start.2 = (f32[4,128]{1,0:T(4,128)S(1)}, f32[4,128]{1,0:T(4,128)}, u32[]{:S(2)}) copy-start(f32[4,128]{1,0:T(4,128)} %get-tuple-element.9) | copy-start | bytes 6148

commit v2 on v1

--- a/solution.py
+++ b/solution.py
@@ -27,10 +27,10 @@
     return j % stride + (j // stride) * 2 * stride
 
 
-def kernel(dims, out_rows, codes, cents, upd, mv2, lognorm,
-           x, cl, cn, s, w, st, gst, nm, norm, ct, cr, sb, rb,
+def kernel(dims, out_rows, codes, cents, lower, num, den, move, lognorm, newlow,
+           x, cl, cn, s, w, st, gst, nm, norm, ct, cr, sb, rb, mv2, pk, gpk, apk,
            bar_l, sem_bs, sem_br, sem_fs, sem_fr, sem_ss, sem_sr,
-           sem_ms, sem_mr, sem_rs, sem_rr, sem_ns, sem_nr):
+           sem_ms, sem_mr, sem_rs, sem_rr, sem_ns, sem_nr, sem_ps, sem_pr, sem_as, sem_ar):
     n_dp, n_mp, feat, ks, sharp, nblk, stride, cols = dims
     group = n_dp // 2
     np_ = 2 * n_mp
@@ -58,13 +58,13 @@
         return {"dp": pick(d, mate_of((core + t) % 2), g), "mp": xor(m, t, n_mp)}
 
     barrier = pltpu.get_barrier_semaphore()
-    partners = [owner(p) for p in range(1, np_)]
+    partners = [owner(p) for p in range(2, np_)]
     partners += [scorer(p) for p in range(1, np_) if p % 2 and (p // 2) % 2]
-    partners += [{"dp": red(j), "mp": m} for j in range(1, group)]
+    partners += [{"dp": xor(d, e, n_dp), "mp": m} for e in range(1, n_dp)]
     for device in partners:
         pl.semaphore_signal(barrier, inc=1, device_id=device, device_id_type=MESH)
 
-    own = pltpu.make_async_copy(out_rows.at[0], x.at[0], bar_l.at[0])
+    own = pltpu.make_async_copy(out_rows.at[m], x.at[0], bar_l.at[0])
     own.start()
     loads = []
     for j in range(group):
@@ -75,7 +75,7 @@
 
     def block_copy(t):
         return pltpu.make_async_remote_copy(
-            src_ref=out_rows.at[t], dst_ref=x.at[2 * t], send_sem=sem_bs.at[t],
+            src_ref=out_rows.at[xor(m, t, n_mp)], dst_ref=x.at[2 * t], send_sem=sem_bs.at[t],
             recv_sem=sem_br.at[t], device_id={"dp": d, "mp": xor(m, t, n_mp)}, device_id_type=MESH)
 
     def forward(t):
@@ -124,10 +124,11 @@
     def score(p):
         prod = lax.dot_general(cl[...], x[p], NT, preferred_element_type=jnp.float32)
         sc = sharp * (2.0 * prod - cn[...])
-        s[p] = sc
         top = jnp.max(sc, axis=0, keepdims=True)
+        ex = jnp.exp(sc - top)
+        s[p] = ex
         st[p, 0:1, :] = top
-        st[p, 1:2, :] = jnp.sum(jnp.exp(sc - top), axis=0, keepdims=True)
+        st[p, 1:2, :] = jnp.sum(ex, axis=0, keepdims=True)
 
     score(0)
 
@@ -149,7 +150,7 @@
     for p in range(1, np_):
         stat_copy(p).wait_recv()
 
-    mine = [codes[t:t + 1, :] for t in range(n_mp)]
+    mine = [codes[pl.ds(xor(m, t, n_mp), 1), :] for t in range(n_mp)]
     slot = [jnp.full((1, BLOCK), -LOW, jnp.float32) for _ in range(n_mp)]
     for b in range(nblk):
         top = jnp.zeros((1, BLOCK), jnp.float32)
@@ -173,7 +174,7 @@
     ct[...] = jnp.zeros_like(ct)
 
     def weigh(p, _):
-        wt = jnp.exp(s[p] - norm[p])
+        wt = s[p] * jnp.exp(st[p, 0:1, :] - norm[p])
         ct[...] += wt
         w[:, pl.ds(pl.multiple_of(p * BLOCK, BLOCK), BLOCK)] = wt.astype(jnp.bfloat16)
         return 0
@@ -208,14 +209,49 @@
             sum_copy(j, c).wait_recv()
             total = total + rb[j - 1, c]
         old = cl[:ks, at].astype(jnp.float32)
-        new = (total + old) / ct[:ks, :1]
-        upd[:, at] = new
+        top = total + old
+        num[:, at] = top
+        new = top / ct[:ks, :1]
         mv2[...] += jnp.broadcast_to(
             jnp.sum(jnp.square(new - old), axis=1, keepdims=True), (ks, BLOCK))
         return 0
 
     lax.fori_loop(0, nc, finish, 0)
-
+    den[...] = ct[:ks]
+    moved = jnp.sqrt(mv2[...] + 1.0)
+    move[...] = moved
+    pk[0] = jnp.max(moved, axis=0, keepdims=True)
+
+    def peak_copy(e):
+        return pltpu.make_async_remote_copy(
+            src_ref=pk.at[0], dst_ref=gpk.at[e], send_sem=sem_ps.at[e], recv_sem=sem_pr.at[e],
+            device_id={"dp": xor(d, e, n_dp), "mp": m}, device_id_type=MESH)
+
+    def shard_copy(t):
+        return pltpu.make_async_remote_copy(
+            src_ref=pk.at[1], dst_ref=apk.at[t], send_sem=sem_as.at[t], recv_sem=sem_ar.at[t],
+            device_id={"dp": d, "mp": xor(m, t, n_mp)}, device_id_type=MESH)
+
+    for e in range(1, n_dp):
+        peak_copy(e).start()
+    best = pk[0]
+    for e in range(1, n_dp):
+        peak_copy(e).wait_recv()
+        best = jnp.maximum(best, gpk[e])
+    pk[1] = best
+    for t in range(1, n_mp):
+        shard_copy(t).start()
+    apk[0] = best
+    for t in range(n_mp):
+        if t:
+            shard_copy(t).wait_recv()
+        row = pl.ds(xor(m, t, n_mp), 1)
+        newlow[row, :] = lower[row, :] - apk[t][:, :1]
+
+    for e in range(1, n_dp):
+        peak_copy(e).wait_send()
+    for t in range(1, n_mp):
+        shard_copy(t).wait_send()
     for p in range(1, np_):
         stat_copy(p).wait_send()
         norm_copy(p).wait_send()
@@ -233,7 +269,6 @@
     n_rows, feat = data_rows.shape
     nblk = n_rows // BLOCK
     n_dp, n_mp = lax.axis_size("dp"), lax.axis_size("mp")
-    m = lax.axis_index("mp")
     ks = centroids.shape[0] // n_dp
     group, np_ = n_dp // 2, 2 * n_mp
     kc = group * ks
@@ -241,24 +276,26 @@
     cols = 512
     nc = feat // cols
     labels = jnp.arange(1, nblk + 1, dtype=jnp.int32)
-    order = jnp.bitwise_xor(jnp.arange(n_mp, dtype=jnp.int32), m)
-    slot_codes = jnp.sum(jnp.take(block_mask, order, axis=0) * labels[None], axis=1)
-    outgoing = jnp.take(data_rows.reshape(nblk, BLOCK, feat), jnp.maximum(slot_codes - 1, 0), axis=0)
+    slot_codes = jnp.sum(block_mask * labels[None], axis=1)
+    picks = jnp.maximum(slot_codes - 1, 0)
+    outgoing = jnp.take(data_rows.reshape(nblk, BLOCK, feat), picks, axis=0, mode="clip")
     codes = jnp.broadcast_to(slot_codes[:, None], (n_mp, BLOCK))
     dims = (n_dp, n_mp, feat, ks, 4.0 / math.sqrt(feat), nblk, stride, cols)
     f32, bf16 = jnp.float32, jnp.bfloat16
     dma = pltpu.SemaphoreType.DMA
     vm = pl.BlockSpec(memory_space=pltpu.VMEM)
     hbm = pl.BlockSpec(memory_space=pl.ANY)
-    upd, mv2, lognorm = pl.pallas_call(
+    num, den, move, lognorm, newlow = pl.pallas_call(
         functools.partial(kernel, dims),
         out_shape=(
             jax.ShapeDtypeStruct((ks, feat), f32),
             jax.ShapeDtypeStruct((ks, BLOCK), f32),
+            jax.ShapeDtypeStruct((ks, BLOCK), f32),
             jax.ShapeDtypeStruct((nblk, BLOCK), f32),
+            jax.ShapeDtypeStruct(lower_bound.shape, f32),
         ),
-        in_specs=[hbm, vm, hbm],
-        out_specs=(vm, vm, vm),
+        in_specs=[hbm, vm, hbm, vm],
+        out_specs=(vm,) * 5,
         scratch_shapes=[
             pltpu.VMEM((np_, BLOCK, feat), bf16),
             pltpu.VMEM((kc, feat), bf16),
@@ -273,6 +310,10 @@
             pltpu.VMEM((group - 1, ks, BLOCK), f32),
             pltpu.VMEM((group - 1, nc, ks, cols), f32),
             pltpu.VMEM((group - 1, nc, ks, cols), f32),
+            pltpu.VMEM((ks, BLOCK), f32),
+            pltpu.VMEM((2, 1, BLOCK), f32),
+            pltpu.VMEM((n_dp, 1, BLOCK), f32),
+            pltpu.VMEM((n_mp, 1, BLOCK), f32),
             dma((1 + group,)),
             dma((n_mp,)), dma((n_mp,)),
             dma((n_mp,)), dma((n_mp,)),
@@ -280,14 +321,13 @@
             dma((np_,)), dma((np_,)),
             dma((group - 1, nc)), dma((group - 1, nc)),
             dma((group - 1,)), dma((group - 1,)),
+            dma((n_dp,)), dma((n_dp,)),
+            dma((n_mp,)), dma((n_mp,)),
         ],
         compiler_params=pltpu.CompilerParams(
             collective_id=0, has_side_effects=True, vmem_limit_bytes=60 * 1024 * 1024),
-    )(outgoing, codes, centroids.reshape(n_dp, ks, feat))
-    movement = jnp.sqrt(mv2[:, 0] + 1.0)
-    shard_peaks = lax.all_gather(jnp.max(movement)[None], ("dp", "mp"), axis=0, tiled=True)
-    shard_peak = jnp.max(shard_peaks.reshape(-1, n_mp), axis=0)
-    return upd, movement, lognorm.reshape(-1), lower_bound - shard_peak[:, None]
+    )(outgoing, codes, centroids.reshape(n_dp, ks, feat), lower_bound)
+    return num / den[:, :1], move[:, 0], lognorm.reshape(-1), newlow
 
 
 def solution(mesh):

time: 214 us -> 178 us (0.83)
  blocking collectives: 38.8 us -> 0 us
  Pallas kernels: 157 us -> 165 us
  other arithmetic: 7.27 us -> 4.77 us
  local copies, waits for them, and re-layouts: 10.2 us -> 7.96 us
    unnamed x1 -> x0, blocking collectives: 38.8 us -> none
    pallas_call x1, Pallas kernels: 157 us -> 165 us  [on_device(): pl.pallas_call(functools.partial(kernel, dims), out_shape=(jax.ShapeDtype...]
    select_n x2 -> x0, other arithmetic: 4.58 us -> none  [the longest x1 4.57 us: on_device(): jnp.take(data_rows.reshape(nblk, BLOCK, feat), jnp.maximum(slot_codes - 1...]
    div x0 -> x1, other arithmetic: none -> 3.99 us  [on_device(): return (num / den[:, :1], move[:, 0], lognorm.reshape(-1), newlow)]
    unnamed x11 -> x8, local copies, waits for them, and re-layouts: 6.16 us -> 2.78 us
where the time goes in v2:
time: 178 us
  Pallas kernels  165 us (93%)
  local copies, waits for them, and re-layouts  7.96 us (4%)
  other arithmetic  4.77 us (3%)
    pallas_call x1, Pallas kernels, on_device(): pl.pallas_call(functools.partial(kernel, dims), out_shape=(jax.ShapeDtype...  165 us
    div x1, other arithmetic, on_device(): return (num / den[:, :1], move[:, 0], lognorm.reshape(-1), newlow)  3.99 us

profile of v2, /device:TPU:0, one launch (start us, length us, event | category | flops | bytes accessed | tf_op | source)
XLA Modules:
  0.0 178.1 jit_solution(11943816081353649356)
XLA Ops:
  0.6 0.0 copy-start
  0.6 1.6 copy-done
  2.2 0.8 multiply_reduce_fusion
  3.0 0.7 broadcast_in_dim.4.codes
  3.7 2.7 %gather_fusion = bf16[8,128,2048]{2,1,0:T(8,128)(2,1)} fusion(bf16[4,128,2048]{2,1,0:T(8,128)(2,1)S(1)} %bitcast.3, s32[1024]{0:T(1024)S(1)} %pad_clamp_fusion), kind=kCustom, calls=%fused_computation | custom fusion | bytes 8388640 | tf_op jit(solution)/shard_map/jit(_take)/gather | solution.py:281
  6.4 164.8 %shard_map.75 = (f32[384,2048]{1,0:T(8,128)}, f32[384,128]{1,0:T(8,128)}, f32[384,128]{1,0:T(8,128)}, f32[4,128]{1,0:T(4,128)}, f32[8,512]{1,0:T(8,128)}) custom-call(bf16[8,128,2048]{2,1,0:T(8,128)(2,1)} %gather_fusion, s32[8,128]{1,0:T(8,128)} %broadcast_in_dim.4.codes, bf16[4,384,2048]{2,1,0:T(8,128)(2,1)} %bitcast.4, f32[8,512]{1,0:T(8,128)} %lower.1), custom_call_target="tpu_custom_call" | custom-call | tf_op jit(solution)/shard_map/pallas_call | solution.py:288
  171.2 1.8 slice_reduce_fusion
  172.9 0.0 copy-start.2
  173.0 0.0 copy-start.1
  173.0 4.0 %broadcast_divide_fusion = f32[384,2048]{1,0:T(8,128)} fusion(f32[384,2048]{1,0:T(8,128)} %get-tuple-element.9, f32[384]{0:T(512)S(1)} %get-tuple-element.15), kind=kLoop, calls=%fused_computation.1 | loop fusion | flops 786432 | bytes 6292992 | tf_op jit(solution)/shard_map/div | solution.py:330
  176.9 0.0 copy-done.2
  176.9 0.6 copy.10
  177.5 0.0 copy-done.1
  177.5 0.6 copy.11
  (3 shorter events, 0.0 us)
Async XLA Ops:
  0.6 1.6 copy-start
  172.9 4.0 %copy-start.2 = (f32[4,128]{1,0:T(4,128)S(1)}, f32[4,128]{1,0:T(4,128)}, u32[]{:S(2)}) copy-start(f32[4,128]{1,0:T(4,128)} %get-tuple-element.12) | copy-start | bytes 6148
  173.0 4.6 %copy-start.1 = (f32[8,512]{1,0:T(8,128)S(1)}, f32[8,512]{1,0:T(8,128)}, u32[]{:S(2)}) copy-start(f32[8,512]{1,0:T(8,128)} %get-tuple-element.23) | copy-start | bytes 49156

commit v3 on v2

--- a/solution.py
+++ b/solution.py
@@ -10,7 +10,10 @@
 
 BLOCK = 128
 SLOTS = 1
+HALVES = 2
 LOW = -1e30
+TINY = 1e-33
+LEVELS = 32767.0
 MESH = pl.DeviceIdType.MESH
 NT = (((1,), (1,)), ((), ()))
 
@@ -28,7 +31,7 @@
 
 
 def kernel(dims, out_rows, codes, cents, lower, num, den, move, lognorm, newlow,
-           x, cl, cn, s, w, st, gst, nm, norm, ct, cr, sb, rb, mv2, pk, gpk, apk,
+           x, cl, cn, s, w, st, gst, nm, norm, ct, cs, cr, pf, sb, rb, mv2, pk, gpk, apk,
            bar_l, sem_bs, sem_br, sem_fs, sem_fr, sem_ss, sem_sr,
            sem_ms, sem_mr, sem_rs, sem_rr, sem_ns, sem_nr, sem_ps, sem_pr, sem_as, sem_ar):
     n_dp, n_mp, feat, ks, sharp, nblk, stride, cols = dims
@@ -73,15 +76,21 @@
         loads.append(c)
     pl.semaphore_wait(barrier, len(partners))
 
-    def block_copy(t):
-        return pltpu.make_async_remote_copy(
-            src_ref=out_rows.at[xor(m, t, n_mp)], dst_ref=x.at[2 * t], send_sem=sem_bs.at[t],
-            recv_sem=sem_br.at[t], device_id={"dp": d, "mp": xor(m, t, n_mp)}, device_id_type=MESH)
-
-    def forward(t):
-        return pltpu.make_async_remote_copy(
-            src_ref=x.at[2 * t], dst_ref=x.at[2 * t + 1], send_sem=sem_fs.at[t],
-            recv_sem=sem_fr.at[t], device_id={"dp": mate, "mp": m}, device_id_type=MESH)
+    half = BLOCK // HALVES
+
+    def block_copy(t, h):
+        part = pl.ds(h * half, half)
+        return pltpu.make_async_remote_copy(
+            src_ref=out_rows.at[xor(m, t, n_mp), part], dst_ref=x.at[2 * t, part],
+            send_sem=sem_bs.at[t, h], recv_sem=sem_br.at[t, h],
+            device_id={"dp": d, "mp": xor(m, t, n_mp)}, device_id_type=MESH)
+
+    def forward(t, h):
+        part = pl.ds(h * half, half)
+        return pltpu.make_async_remote_copy(
+            src_ref=x.at[2 * t, part], dst_ref=x.at[2 * t + 1, part],
+            send_sem=sem_fs.at[t, h], recv_sem=sem_fr.at[t, h],
+            device_id={"dp": mate, "mp": m}, device_id_type=MESH)
 
     def stat_copy(p):
         return pltpu.make_async_remote_copy(
@@ -100,11 +109,12 @@
 
     def count_copy(j):
         return pltpu.make_async_remote_copy(
-            src_ref=ct.at[pl.ds(j * ks, ks)], dst_ref=cr.at[j - 1], send_sem=sem_ns.at[j - 1],
+            src_ref=cs.at[j - 1], dst_ref=cr.at[j - 1], send_sem=sem_ns.at[j - 1],
             recv_sem=sem_nr.at[j - 1], device_id={"dp": red(j), "mp": m}, device_id_type=MESH)
 
     for t in range(1, n_mp):
-        block_copy(t).start()
+        for h in range(HALVES):
+            block_copy(t, h).start()
 
     for c in loads:
         c.wait()
@@ -118,7 +128,8 @@
         cn[r, :] = jnp.broadcast_to(jnp.sum(v * v, axis=1, keepdims=True), (step, BLOCK))
         return 0
 
-    forward(0).start()
+    for h in range(HALVES):
+        forward(0, h).start()
     lax.fori_loop(0, cl.shape[0] // step, norm_rows, 0)
 
     def score(p):
@@ -135,12 +146,14 @@
     def body(i, _):
         @pl.when(i < n_mp)
         def _():
-            block_copy(i).wait_recv()
-            forward(i).start()
+            for h in range(HALVES):
+                block_copy(i, h).wait_recv()
+                forward(i, h).start()
             score(2 * i)
             stat_copy(2 * i).start()
 
-        forward(i - 1).wait_recv()
+        for h in range(HALVES):
+            forward(i - 1, h).wait_recv()
         score(2 * i - 1)
         stat_copy(2 * i - 1).start()
         return 0
@@ -186,20 +199,31 @@
         return jnp.dot(w[j * ks:(j + 1) * ks, :], x[:, :, at].reshape(np_ * BLOCK, cols),
                        preferred_element_type=jnp.float32)
 
+    lane = lax.broadcasted_iota(jnp.int32, (ks, BLOCK), 1)
     for j in range(1, group):
+        def build(c, peak):
+            val = partial(j, c)
+            pf[c] = val
+            return jnp.maximum(peak, jnp.max(jnp.abs(val), axis=1, keepdims=True))
+
+        peak = lax.fori_loop(0, nc, build, jnp.full((ks, 1), TINY, jnp.float32))
+        tally = jnp.sum(ct[j * ks:(j + 1) * ks], axis=1, keepdims=True)
+        cs[j - 1] = jnp.where(lane < BLOCK // 2, tally, peak * (1.0 / LEVELS))
         count_copy(j).start()
+        mv2[...] = jnp.broadcast_to(LEVELS / peak, (ks, BLOCK))
 
         def send(c, _):
-            sb[j - 1, c] = partial(j, c)
+            level = jnp.clip(jnp.round(pf[c] * mv2[:, :1]), -LEVELS, LEVELS)
+            sb[j - 1, c] = level.astype(jnp.int32).astype(jnp.int16)
             sum_copy(j, c).start()
             return 0
 
         lax.fori_loop(0, nc, send, 0)
-    cnt = ct[:ks]
+    cnt = jnp.sum(ct[:ks], axis=1, keepdims=True) + 1.0
     for j in range(1, group):
         count_copy(j).wait_recv()
-        cnt = cnt + cr[j - 1]
-    ct[:ks] = jnp.broadcast_to(jnp.sum(cnt, axis=1, keepdims=True) + 1.0, (ks, BLOCK))
+        cnt = cnt + cr[j - 1, :, :1]
+    ct[:ks] = jnp.broadcast_to(cnt, (ks, BLOCK))
     mv2[...] = jnp.zeros_like(mv2)
 
     def finish(c, _):
@@ -207,7 +231,7 @@
         total = partial(0, c)
         for j in range(1, group):
             sum_copy(j, c).wait_recv()
-            total = total + rb[j - 1, c]
+            total = total + rb[j - 1, c].astype(jnp.int32).astype(jnp.float32) * cr[j - 1, :, BLOCK - 1:]
         old = cl[:ks, at].astype(jnp.float32)
         top = total + old
         num[:, at] = top
@@ -256,9 +280,10 @@
         stat_copy(p).wait_send()
         norm_copy(p).wait_send()
     for t in range(n_mp):
-        if t:
-            block_copy(t).wait_send()
-        forward(t).wait_send()
+        for h in range(HALVES):
+            if t:
+                block_copy(t, h).wait_send()
+            forward(t, h).wait_send()
     for j in range(1, group):
         count_copy(j).wait_send()
         for c in range(nc):
@@ -273,7 +298,7 @@
     group, np_ = n_dp // 2, 2 * n_mp
     kc = group * ks
     stride = math.isqrt(n_dp)
-    cols = 512
+    cols = 256
     nc = feat // cols
     labels = jnp.arange(1, nblk + 1, dtype=jnp.int32)
     slot_codes = jnp.sum(block_mask * labels[None], axis=1)
@@ -284,7 +309,7 @@
     f32, bf16 = jnp.float32, jnp.bfloat16
     dma = pltpu.SemaphoreType.DMA
     vm = pl.BlockSpec(memory_space=pltpu.VMEM)
-    hbm = pl.BlockSpec(memory_space=pl.ANY)
+    hbm = pl.BlockSpec(memory_space=pltpu.HBM)
     num, den, move, lognorm, newlow = pl.pallas_call(
         functools.partial(kernel, dims),
         out_shape=(
@@ -308,15 +333,17 @@
             pltpu.VMEM((np_, 1, BLOCK), f32),
             pltpu.VMEM((kc, BLOCK), f32),
             pltpu.VMEM((group - 1, ks, BLOCK), f32),
-            pltpu.VMEM((group - 1, nc, ks, cols), f32),
-            pltpu.VMEM((group - 1, nc, ks, cols), f32),
+            pltpu.VMEM((group - 1, ks, BLOCK), f32),
+            pltpu.VMEM((nc, ks, cols), f32),
+            pltpu.VMEM((group - 1, nc, ks, cols), jnp.int16),
+            pltpu.VMEM((group - 1, nc, ks, cols), jnp.int16),
             pltpu.VMEM((ks, BLOCK), f32),
             pltpu.VMEM((2, 1, BLOCK), f32),
             pltpu.VMEM((n_dp, 1, BLOCK), f32),
             pltpu.VMEM((n_mp, 1, BLOCK), f32),
             dma((1 + group,)),
-            dma((n_mp,)), dma((n_mp,)),
-            dma((n_mp,)), dma((n_mp,)),
+            dma((n_mp, HALVES)), dma((n_mp, HALVES)),
+            dma((n_mp, HALVES)), dma((n_mp, HALVES)),
             dma((np_,)), dma((np_,)),
             dma((np_,)), dma((np_,)),
             dma((group - 1, nc)), dma((group - 1, nc)),
@@ -325,7 +352,7 @@
             dma((n_mp,)), dma((n_mp,)),
         ],
         compiler_params=pltpu.CompilerParams(
-            collective_id=0, has_side_effects=True, vmem_limit_bytes=60 * 1024 * 1024),
+            collective_id=0, has_side_effects=True, vmem_limit_bytes=44 * 1024 * 1024),
     )(outgoing, codes, centroids.reshape(n_dp, ks, feat), lower_bound)
     return num / den[:, :1], move[:, 0], lognorm.reshape(-1), newlow
 

time: 178 us -> 160 us (0.90)
  Pallas kernels: 165 us -> 148 us
  other arithmetic: 4.77 us -> 2.79 us
    pallas_call x1, Pallas kernels: 165 us -> 148 us  [on_device(): pl.pallas_call(functools.partial(kernel, dims), out_shape=(jax.ShapeDtype...]
    unnamed x8, local copies, waits for them, and re-layouts: 2.78 us -> 4.96 us
    div x1, other arithmetic: 3.99 us -> 2.01 us  [on_device(): return (num / den[:, :1], move[:, 0], lognorm.reshape(-1), newlow)]
where the time goes in v3:
time: 160 us
  Pallas kernels  148 us (92%)
  local copies, waits for them, and re-layouts  8.5 us (5%)
  other arithmetic  2.79 us (2%)
    pallas_call x1, Pallas kernels, on_device(): pl.pallas_call(functools.partial(kernel, dims), out_shape=(jax.ShapeDtype...  148 us
    unnamed x8, local copies, waits for them, and re-layouts  4.96 us

profile of v3, /device:TPU:0, one launch (start us, length us, event | category | flops | bytes accessed | tf_op | source)
XLA Modules:
  0.0 159.8 jit_solution(5058332062140884363)
XLA Ops:
  0.6 0.0 copy-start
  0.6 1.6 copy-done
  2.2 0.8 multiply_reduce_fusion
  3.0 0.1 broadcast_in_dim.4.codes
  3.1 0.0 copy-start.2
  3.1 2.7 %gather_fusion = bf16[8,128,2048]{2,1,0:T(8,128)(2,1)} fusion(bf16[4,128,2048]{2,1,0:T(8,128)(2,1)S(1)} %bitcast.3, s32[1024]{0:T(1024)S(1)} %pad_clamp_fusion), kind=kCustom, calls=%fused_computation | custom fusion | bytes 8388640 | tf_op jit(solution)/shard_map/jit(_take)/gather | solution.py:306
  5.8 0.0 copy-done.2
  5.8 0.0 copy-start.1
  5.8 2.2 %copy-done.1 = bf16[8,128,2048]{2,1,0:T(8,128)(2,1)S(1)} copy-done((bf16[8,128,2048]{2,1,0:T(8,128)(2,1)S(1)}, bf16[8,128,2048]{2,1,0:T(8,128)(2,1)}, u32[]{:S(2)}) %copy-start.1) | copy-done | bytes 4194328
  8.0 147.8 %shard_map.75 = (f32[384,2048]{1,0:T(8,128)S(1)}, f32[384,128]{1,0:T(8,128)S(1)}, f32[384,128]{1,0:T(8,128)S(1)}, f32[4,128]{1,0:T(4,128)S(1)}, f32[8,512]{1,0:T(8,128)S(1)}) custom-call(bf16[8,128,2048]{2,1,0:T(8,128)(2,1)S(1)} %copy-done.1, s32[8,128]{1,0:T(8,128)S(1)} %broadcast_in_dim.4.codes, bf16[4,384,2048]{2,1,0:T(8,128)(2,1)} %bitcast.5, ...), custom_call_target="tpu_custom_call" | custom-call | tf_op jit(solution)/shard_map/pallas_call | solution.py:313
  155.8 0.7 slice_reduce_fusion
  156.6 2.0 %broadcast_divide_fusion = f32[384,2048]{1,0:T(8,128)} fusion(f32[384,2048]{1,0:T(8,128)S(1)} %get-tuple-element.9, f32[384]{0:T(512)S(1)} %get-tuple-element.15), kind=kLoop, calls=%fused_computation.1 | loop fusion | flops 786432 | bytes 6292992 | tf_op jit(solution)/shard_map/div | solution.py:357
  158.6 0.6 copy.10
  159.2 0.6 copy.11
  (3 shorter events, 0.0 us)
Async XLA Ops:
  0.6 1.6 copy-start
  3.1 2.7 %copy-start.2 = (f32[8,512]{1,0:T(8,128)S(1)}, f32[8,512]{1,0:T(8,128)}, u32[]{:S(2)}) copy-start(f32[8,512]{1,0:T(8,128)} %lower.1) | copy-start | bytes 49156
  5.8 2.2 %copy-start.1 = (bf16[8,128,2048]{2,1,0:T(8,128)(2,1)S(1)}, bf16[8,128,2048]{2,1,0:T(8,128)(2,1)}, u32[]{:S(2)}) copy-start(bf16[8,128,2048]{2,1,0:T(8,128)(2,1)} %gather_fusion) | copy-start | bytes 12582916

commit v4 on v3

--- a/solution.py
+++ b/solution.py
@@ -10,7 +10,7 @@
 
 BLOCK = 128
 SLOTS = 1
-HALVES = 2
+HALVES = 4
 LOW = -1e30
 TINY = 1e-33
 LEVELS = 32767.0
@@ -186,13 +186,16 @@
 
     ct[...] = jnp.zeros_like(ct)
 
-    def weigh(p, _):
-        wt = s[p] * jnp.exp(st[p, 0:1, :] - norm[p])
-        ct[...] += wt
-        w[:, pl.ds(pl.multiple_of(p * BLOCK, BLOCK), BLOCK)] = wt.astype(jnp.bfloat16)
-        return 0
-
-    lax.fori_loop(0, np_, weigh, 0)
+    def weigh(j):
+        rows = pl.ds(j * ks, ks)
+
+        def one(p, _):
+            wt = s[p, rows, :] * jnp.exp(st[p, 0:1, :] - norm[p])
+            ct[rows, :] += wt
+            w[rows, pl.ds(pl.multiple_of(p * BLOCK, BLOCK), BLOCK)] = wt.astype(jnp.bfloat16)
+            return 0
+
+        lax.fori_loop(0, np_, one, 0)
 
     def partial(j, c):
         at = pl.ds(pl.multiple_of(c * cols, cols), cols)
@@ -206,6 +209,7 @@
             pf[c] = val
             return jnp.maximum(peak, jnp.max(jnp.abs(val), axis=1, keepdims=True))
 
+        weigh(j)
         peak = lax.fori_loop(0, nc, build, jnp.full((ks, 1), TINY, jnp.float32))
         tally = jnp.sum(ct[j * ks:(j + 1) * ks], axis=1, keepdims=True)
         cs[j - 1] = jnp.where(lane < BLOCK // 2, tally, peak * (1.0 / LEVELS))
@@ -219,6 +223,7 @@
             return 0
 
         lax.fori_loop(0, nc, send, 0)
+    weigh(0)
     cnt = jnp.sum(ct[:ks], axis=1, keepdims=True) + 1.0
     for j in range(1, group):
         count_copy(j).wait_recv()

time: 160 us -> 158 us (0.988)
  Pallas kernels: 148 us -> 146 us
    pallas_call x1, Pallas kernels: 148 us -> 146 us  [on_device(): pl.pallas_call(functools.partial(kernel, dims), out_shape=(jax.ShapeDtype...]
where the time goes in v4:
time: 158 us
  Pallas kernels  146 us (92%)
  local copies, waits for them, and re-layouts  8.5 us (5%)
  other arithmetic  2.79 us (2%)
    pallas_call x1, Pallas kernels, on_device(): pl.pallas_call(functools.partial(kernel, dims), out_shape=(jax.ShapeDtype...  146 us
    unnamed x8, local copies, waits for them, and re-layouts  4.96 us

profile of v4, /device:TPU:0, one launch (start us, length us, event | category | flops | bytes accessed | tf_op | source)
XLA Modules:
  0.0 158.2 jit_solution(3807548359706942361)
XLA Ops:
  0.6 0.0 copy-start
  0.6 1.6 %copy-done = bf16[512,2048]{1,0:T(8,128)(2,1)S(1)} copy-done((bf16[512,2048]{1,0:T(8,128)(2,1)S(1)}, bf16[512,2048]{1,0:T(8,128)(2,1)}, u32[]{:S(2)}) %copy-start) | copy-done | bytes 2097176
  2.2 0.8 multiply_reduce_fusion
  3.0 0.1 broadcast_in_dim.4.codes
  3.1 0.0 copy-start.2
  3.1 2.7 %gather_fusion = bf16[8,128,2048]{2,1,0:T(8,128)(2,1)} fusion(bf16[4,128,2048]{2,1,0:T(8,128)(2,1)S(1)} %bitcast.3, s32[1024]{0:T(1024)S(1)} %pad_clamp_fusion), kind=kCustom, calls=%fused_computation | custom fusion | bytes 8388640 | tf_op jit(solution)/shard_map/jit(_take)/gather | solution.py:311
  5.8 0.0 copy-done.2
  5.8 0.0 copy-start.1
  5.8 2.2 %copy-done.1 = bf16[8,128,2048]{2,1,0:T(8,128)(2,1)S(1)} copy-done((bf16[8,128,2048]{2,1,0:T(8,128)(2,1)S(1)}, bf16[8,128,2048]{2,1,0:T(8,128)(2,1)}, u32[]{:S(2)}) %copy-start.1) | copy-done | bytes 4194328
  8.0 146.2 %shard_map.75 = (f32[384,2048]{1,0:T(8,128)S(1)}, f32[384,128]{1,0:T(8,128)S(1)}, f32[384,128]{1,0:T(8,128)S(1)}, f32[4,128]{1,0:T(4,128)S(1)}, f32[8,512]{1,0:T(8,128)S(1)}) custom-call(bf16[8,128,2048]{2,1,0:T(8,128)(2,1)S(1)} %copy-done.1, s32[8,128]{1,0:T(8,128)S(1)} %broadcast_in_dim.4.codes, bf16[4,384,2048]{2,1,0:T(8,128)(2,1)} %bitcast.5, ...), custom_call_target="tpu_custom_call" | custom-call | tf_op jit(solution)/shard_map/pallas_call | solution.py:318
  154.2 0.7 slice_reduce_fusion
  155.0 2.0 %broadcast_divide_fusion = f32[384,2048]{1,0:T(8,128)} fusion(f32[384,2048]{1,0:T(8,128)S(1)} %get-tuple-element.9, f32[384]{0:T(512)S(1)} %get-tuple-element.15), kind=kLoop, calls=%fused_computation.1 | loop fusion | flops 786432 | bytes 6292992 | tf_op jit(solution)/shard_map/div | solution.py:362
  157.0 0.6 copy.10
  157.6 0.6 copy.11
  (3 shorter events, 0.0 us)
Async XLA Ops:
  0.6 1.6 %copy-start = (bf16[512,2048]{1,0:T(8,128)(2,1)S(1)}, bf16[512,2048]{1,0:T(8,128)(2,1)}, u32[]{:S(2)}) copy-start(bf16[512,2048]{1,0:T(8,128)(2,1)} %param.4) | copy-start | bytes 6291460
  3.1 2.7 %copy-start.2 = (f32[8,512]{1,0:T(8,128)S(1)}, f32[8,512]{1,0:T(8,128)}, u32[]{:S(2)}) copy-start(f32[8,512]{1,0:T(8,128)} %lower.1) | copy-start | bytes 49156
  5.8 2.2 %copy-start.1 = (bf16[8,128,2048]{2,1,0:T(8,128)(2,1)S(1)}, bf16[8,128,2048]{2,1,0:T(8,128)(2,1)}, u32[]{:S(2)}) copy-start(bf16[8,128,2048]{2,1,0:T(8,128)(2,1)} %gather_fusion) | copy-start | bytes 12582916
